TPU v7x, 32 devices: a whole 2x2x4 slice. The times are simulated.
32 devices in a mesh: col: 4 (over y, core), row: 8 (over z, x).
Axes of the slice: x: 2, y: 2, z: 4, core: 2. Of those that a mesh axis runs over, the one named last changes fastest.
Arguments:
- column_table: float32 [32768, 512], P('row', 'col'), may hold values from -3 to 3
- bag_rows: int32 [256, 32], P('row'), may hold values from 0 to 32767
Outputs:
- row_table: float32 [8, 4096, 512], P(None, ('col', 'row'))
- pooled: float32 [256, 512], P('row', 'col')
Inputs may be any that keep to these rules, and one draw needn't show every extreme that they name: `bag_rows`: row indices of the table; a few rows are named far more often than the rest.
All inputs are finite; a program needn't handle non-finite values.
Results may differ from a plain program's by a relative error of at most 0.000078.
Values sent between devices are 32-bit elements; how exact they have to be, the bound alone decides.
A program may use at most 64 MiB of HBM per device.

v0:
```python
import math

import jax
import jax.numpy as jnp
from jax import lax
from jax.sharding import PartitionSpec as P


def pooling(positions, table_rows):
    row_count = table_rows.shape[0]
    bag_count = positions.shape[0]
    block_rows = math.gcd(row_count, 512)
    turns = row_count // block_rows
    running = jnp.zeros((bag_count, table_rows.shape[1]), jnp.float32)
    tile_ids = jnp.arange(block_rows, dtype=jnp.int32)

    def advance(turn, carried):
        offset = turn * block_rows
        within = positions - offset
        matches = within[:, :, None] == tile_ids[None, None, :]
        counts = jnp.sum(matches.astype(jnp.float32), axis=1)
        table_block = lax.dynamic_slice_in_dim(table_rows, offset, block_rows, 0)
        return carried + jnp.dot(
            counts, table_block, precision=lax.Precision.HIGHEST, preferred_element_type=jnp.float32
        )

    return lax.fori_loop(0, turns, advance, running)


def per_device(column_table, bag_rows):
    row_groups = lax.axis_size("row")
    col_groups = lax.axis_size("col")
    block_len, col_width = column_table.shape
    full_width = col_width * col_groups
    span = block_len // (col_groups * row_groups)
    row_index = lax.axis_index("row")
    every_bag = lax.all_gather(bag_rows, "row", axis=0, tiled=True)
    sectioned = column_table.reshape(col_groups, row_groups, span, col_width)
    moved = lax.all_to_all(
        lax.all_to_all(sectioned, "col", split_axis=0, concat_axis=3, tiled=True),
        "row",
        split_axis=1,
        concat_axis=0,
        tiled=True,
    )
    row_table = moved.reshape(row_groups, span, full_width)
    first_row = row_index * block_len
    shifted = every_bag - first_row
    inside = (shifted >= 0) & (shifted < block_len)
    positions = jnp.where(inside, shifted, -1)
    pooled = lax.psum_scatter(
        pooling(positions, column_table), "row", scatter_dimension=0, tiled=True
    )
    return (row_table, pooled)


def solution(mesh):
    return jax.shard_map(
        per_device,
        mesh=mesh,
        in_specs=(P("row", "col"), P("row", None)),
        out_specs=(P(None, ("col", "row"), None), P("row", "col")),
        check_vma=False,
    )
```

profile of v0, /device:TPU:0, one launch (start us, length us, event | category | flops | bytes accessed | tf_op | source)
XLA Modules:
  0.0 161.4 jit_solution(9347695507978795825)
XLA Ops:
  7.2 0.0 copy-start.1
  7.2 4.3 %all-to-all-start = ((f32[4,8,128,128]{3,2,1,0:T(8,128)}), f32[4,8,128,128]{3,2,1,0:T(8,128)S(1)}, u32[]{:S(2)}, u32[]{:S(2)}) async-start(f32[4,8,128,128]{3,2,1,0:T(8,128)} %bitcast.12), calls=%async_computation | async-start | bytes 4194304 | tf_op jit(solution)/shard_map/all_to_all | solution.py:40
  11.5 0.0 copy-done.1
  11.5 31.8 %all_gather.3 = s32[256,32]{1,0:T(8,128)S(1)} all-gather(s32[32,32]{1,0:T(8,128)S(1)} %copy-done.1), channel_id=1, replica_groups=mesh['col'=4,'row'=8] {'row'}, dimensions={0}, use_global_device_ids=true | all-gather | bytes 36864 | tf_op jit(solution)/shard_map/all_gather | solution.py:37
  43.3 0.0 all-to-all-done
  43.3 1.8 %copy.7 = f32[4,8,128,128]{2,3,0,1:T(8,128)} copy(f32[4,8,128,128]{3,2,1,0:T(8,128)S(1)} %all-to-all-done) | data formatting | bytes 4194304 | tf_op jit(solution)/shard_map/all_to_all | solution.py:40
  45.1 2.9 %copy.8 = f32[1,8,128,512]{3,2,0,1:T(8,128)} copy(f32[1,8,128,512]{2,3,1,0:T(8,128)} %bitcast.11) | data formatting | bytes 4194304 | tf_op jit(solution)/shard_map/all_to_all | solution.py:40
  48.0 5.4 %all-to-all-start.1 = ((f32[1,8,128,512]{3,2,0,1:T(8,128)}), f32[1,8,128,512]{3,2,0,1:T(8,128)S(1)}, u32[]{:S(2)}, u32[]{:S(2)}) async-start(f32[1,8,128,512]{3,2,0,1:T(8,128)} %copy.8), calls=%async_computation.1 | async-start | bytes 4194304 | tf_op jit(solution)/shard_map/all_to_all | solution.py:39
  53.4 0.0 reduce-scatter.2.cloned.1.call-start
  53.4 35.3 %while.14 = (s32[]{:T(128)}, f32[256,128]{1,0:T(8,128)S(1)}, s32[256,32]{1,0:T(8,128)S(1)}, f32[4096,128]{1,0:T(8,128)}, s32[]{:T(128)}, /*index=5*/s32[]{:T(128)}, s32[]{:T(128)}, s32[]{:T(128)}) while((s32[]{:T(128)}, f32[256,128]{1,0:T(8,128)S(1)}, s32[256,32]{1,0:T(8,128)S(1)}, f32[4096,128]{1,0:T(8,128)}, s32[]{:T(128)}, ...), condition=%wide.region_2.3_spmd.clone, body=%wide.region_0.2_spmd.clone.sunk | while | flops 213852160 | bytes 1671317 | solution.py:27
  53.5 2.8 %convert_reduce_fusion.2 = f32[256,512]{1,0:T(8,128)S(1)} fusion(s32[256,32]{1,0:T(8,128)S(1)} %broadcast_subtract_fusion.2), kind=kLoop, calls=%fused_computation.2.clone.1 | loop fusion | flops 12451840 | bytes 557056 | tf_op jit(solution)/shard_map/while/body/eval_jaxpr/reduce_sum | solution.py:21
  56.3 1.6 convolution_add_fusion.2
  57.9 2.8 %convert_reduce_fusion.2 = f32[256,512]{1,0:T(8,128)S(1)} fusion(s32[256,32]{1,0:T(8,128)S(1)} %broadcast_subtract_fusion.2), kind=kLoop, calls=%fused_computation.2.clone.1 | loop fusion | flops 12451840 | bytes 557056 | tf_op jit(solution)/shard_map/while/body/eval_jaxpr/reduce_sum | solution.py:21
  60.7 1.6 convolution_add_fusion.2
  62.3 2.8 %convert_reduce_fusion.2 = f32[256,512]{1,0:T(8,128)S(1)} fusion(s32[256,32]{1,0:T(8,128)S(1)} %broadcast_subtract_fusion.2), kind=kLoop, calls=%fused_computation.2.clone.1 | loop fusion | flops 12451840 | bytes 557056 | tf_op jit(solution)/shard_map/while/body/eval_jaxpr/reduce_sum | solution.py:21
  65.1 1.6 convolution_add_fusion.2
  66.7 2.8 %convert_reduce_fusion.2 = f32[256,512]{1,0:T(8,128)S(1)} fusion(s32[256,32]{1,0:T(8,128)S(1)} %broadcast_subtract_fusion.2), kind=kLoop, calls=%fused_computation.2.clone.1 | loop fusion | flops 12451840 | bytes 557056 | tf_op jit(solution)/shard_map/while/body/eval_jaxpr/reduce_sum | solution.py:21
  69.5 1.6 convolution_add_fusion.2
  71.1 2.8 %convert_reduce_fusion.2 = f32[256,512]{1,0:T(8,128)S(1)} fusion(s32[256,32]{1,0:T(8,128)S(1)} %broadcast_subtract_fusion.2), kind=kLoop, calls=%fused_computation.2.clone.1 | loop fusion | flops 12451840 | bytes 557056 | tf_op jit(solution)/shard_map/while/body/eval_jaxpr/reduce_sum | solution.py:21
  73.9 1.6 convolution_add_fusion.2
  75.5 2.8 %convert_reduce_fusion.2 = f32[256,512]{1,0:T(8,128)S(1)} fusion(s32[256,32]{1,0:T(8,128)S(1)} %broadcast_subtract_fusion.2), kind=kLoop, calls=%fused_computation.2.clone.1 | loop fusion | flops 12451840 | bytes 557056 | tf_op jit(solution)/shard_map/while/body/eval_jaxpr/reduce_sum | solution.py:21
  78.3 1.6 convolution_add_fusion.2
  79.9 2.8 %convert_reduce_fusion.2 = f32[256,512]{1,0:T(8,128)S(1)} fusion(s32[256,32]{1,0:T(8,128)S(1)} %broadcast_subtract_fusion.2), kind=kLoop, calls=%fused_computation.2.clone.1 | loop fusion | flops 12451840 | bytes 557056 | tf_op jit(solution)/shard_map/while/body/eval_jaxpr/reduce_sum | solution.py:21
  82.7 1.6 convolution_add_fusion.2
  84.3 2.8 %convert_reduce_fusion.2 = f32[256,512]{1,0:T(8,128)S(1)} fusion(s32[256,32]{1,0:T(8,128)S(1)} %broadcast_subtract_fusion.2), kind=kLoop, calls=%fused_computation.2.clone.1 | loop fusion | flops 12451840 | bytes 557056 | tf_op jit(solution)/shard_map/while/body/eval_jaxpr/reduce_sum | solution.py:21
  87.1 1.6 convolution_add_fusion.2
  88.7 0.0 copy-start
  88.7 0.6 copy-done
  89.4 0.0 reduce-scatter.2.cloned.1.call-update
  89.4 7.2 %all-to-all-done.1 = f32[1,8,128,512]{3,2,0,1:T(8,128)S(1)} async-done(((f32[1,8,128,512]{3,2,0,1:T(8,128)}), f32[1,8,128,512]{3,2,0,1:T(8,128)S(1)}, u32[]{:S(2)}, u32[]{:S(2)}) %all-to-all-start.1) | async-done | bytes 2097184 | tf_op jit(solution)/shard_map/all_to_all | solution.py:39
  96.6 56.6 %reduce-scatter.2.cloned.1.call-done = f32[32,128]{1,0:T(8,128)} async-done(((f32[256,128]{1,0:T(8,128)}), f32[32,128]{1,0:T(8,128)}) %reduce-scatter.2.cloned.1.call-update) | async-done | bytes 16400 | tf_op jit(solution)/shard_map/reduce_scatter | solution.py:51
  153.2 1.3 copy.16
  (10 shorter events, 0.1 us)
Async XLA Ops:
  7.2 4.3 %copy-start.1 = (s32[32,32]{1,0:T(8,128)S(1)}, s32[32,32]{1,0:T(8,128)}, u32[]{:S(2)}) copy-start(s32[32,32]{1,0:T(8,128)} %param.5) | copy-start | bytes 12292
  7.2 36.1 %all-to-all-start = ((f32[4,8,128,128]{3,2,1,0:T(8,128)}), f32[4,8,128,128]{3,2,1,0:T(8,128)S(1)}, u32[]{:S(2)}, u32[]{:S(2)}) async-start(f32[4,8,128,128]{3,2,1,0:T(8,128)} %bitcast.12), calls=%async_computation | async-start | bytes 4194304 | tf_op jit(solution)/shard_map/all_to_all | solution.py:40
  48.0 48.6 %all-to-all-start.1 = ((f32[1,8,128,512]{3,2,0,1:T(8,128)}), f32[1,8,128,512]{3,2,0,1:T(8,128)S(1)}, u32[]{:S(2)}, u32[]{:S(2)}) async-start(f32[1,8,128,512]{3,2,0,1:T(8,128)} %copy.8), calls=%async_computation.1 | async-start | bytes 4194304 | tf_op jit(solution)/shard_map/all_to_all | solution.py:39
  53.4 99.8 %reduce-scatter.2.cloned.1.call-start = ((), (), s32[]{:S(2)}) async-start(), calls=%async_computation.3 | async-start | bytes 147456 | tf_op jit(solution)/shard_map/reduce_scatter | solution.py:51
  88.7 0.7 copy-start
Sparse Core Ops, SparseCore 0:
  89.5 63.6 reduce-scatter.1
where the time goes:
time: 162 us; the launch traced here: 161 us
  waiting for transfers between devices  63.8 us (39%)
  blocking collectives  31.8 us (20%)
  other arithmetic  22.3 us (14%)
  between operations  14.1 us (9%)
  matrix products  12.6 us (8%)
  starting transfers between devices  9.69 us (6%)
  local copies, waits for them, and re-layouts  6.71 us (4%)
    reduce_scatter x1, waiting for transfers between devices, per_device(): lax.psum_scatter(pooling(positions, column_table), 'row', scatter_dimensi...  56.6 us
    all_gather x1, blocking collectives, per_device(): every_bag = lax.all_gather(bag_rows, 'row', axis=0, tiled=True)  31.8 us
    reduce_sum x8, other arithmetic, advance(): counts = jnp.sum(matches.astype(jnp.float32), axis=1)  22.2 us
    dot_general x8, matrix products, advance(): jnp.dot(counts, table_block, precision=lax.Precision.HIGHEST, preferred_e...  12.6 us
    all_to_all x1, waiting for transfers between devices, per_device(): lax.all_to_all(lax.all_to_all(sectioned, 'col', split_axis=0, concat_axis...  7.22 us
    all_to_all x1, starting transfers between devices, per_device(): lax.all_to_all(lax.all_to_all(sectioned, 'col', split_axis=0, concat_axis...  5.38 us
    all_to_all x2, local copies, waits for them, and re-layouts, per_device(): lax.all_to_all(sectioned, 'col', split_axis=0, concat_axis=3, tiled=True)  4.73 us
    all_to_all x1, starting transfers between devices, per_device(): lax.all_to_all(sectioned, 'col', split_axis=0, concat_axis=3, tiled=True)  4.28 us
  transfers between devices with their start and end apart: 3, of which 2 were waited for; matrix products, arithmetic and copies ran while one was open for 22% of the time, Pallas kernels for 0%

commit v1 on v0

--- a/solution.py
+++ b/solution.py
@@ -1,9 +1,16 @@
+import functools
 import math
 
 import jax
 import jax.numpy as jnp
 from jax import lax
+from jax.experimental import pallas as pl
+from jax.experimental.pallas import tpu as pltpu
 from jax.sharding import PartitionSpec as P
+
+MESH = pl.DeviceIdType.MESH
+LANES = 128
+SUBLANES = 8
 
 
 def pooling(positions, table_rows):
@@ -27,7 +34,7 @@
     return lax.fori_loop(0, turns, advance, running)
 
 
-def per_device(column_table, bag_rows):
+def general(column_table, bag_rows):
     row_groups = lax.axis_size("row")
     col_groups = lax.axis_size("col")
     block_len, col_width = column_table.shape
@@ -54,6 +61,190 @@
     return (row_table, pooled)
 
 
+def flipped(index, mask, count):
+    result, bit = 0, 1
+    while bit < count:
+        digit = lax.rem(lax.div(index, bit), 2)
+        result = result + (1 - digit if mask & bit else digit) * bit
+        bit *= 2
+    return result
+
+
+def kernel(
+    row_groups, col_groups,
+    table_ref, bags_ref, out_ref, pooled_ref,
+    table_v, packed, gathered, counts, partial, arrived,
+    load_sem, own_sem, send_sem, recv_sem, bag_send, bag_recv, sum_send, sum_recv,
+):
+    rows, cols = row_groups, col_groups
+    r, c = lax.axis_index("row"), lax.axis_index("col")
+    block_len, width = table_ref.shape
+    span = block_len // (rows * cols)
+    own_bags, bag_len = bags_ref.shape
+    per_vreg = LANES // bag_len
+    flat = c * rows + r
+
+    load = pltpu.make_async_copy(table_ref, table_v, load_sem)
+    load.start()
+    lane0 = pl.multiple_of(c * width, width)
+    own = pltpu.make_async_copy(
+        table_ref.at[pl.ds(flat * span, span), :],
+        out_ref.at[r, :, pl.ds(lane0, width)],
+        own_sem,
+    )
+    own.start()
+
+    tile_bags = own_bags // per_vreg
+    packed[...] = jnp.concatenate(
+        [bags_ref[q * tile_bags:(q + 1) * tile_bags, :] for q in range(per_vreg)], axis=1
+    )
+    gathered[r] = packed[...]
+
+    masks = [(mr, mc) for mr in range(rows) for mc in range(cols) if (mr, mc) != (0, 0)]
+    far = [m for m in masks if m[0] >= rows // 2]
+    near = [m for m in masks if m[0] < rows // 2]
+    far = sorted(far, key=lambda m: -m[0])
+    near = sorted(near, key=lambda m: -m[0])
+    order = ORDER(far, near)
+
+    def peer(mr, mc):
+        return flipped(r, mr, rows), flipped(c, mc, cols)
+
+    barrier = pltpu.get_barrier_semaphore()
+    for mr, mc in order:
+        pr, pc = peer(mr, mc)
+        pl.semaphore_signal(barrier, inc=1, device_id=(pc, pr), device_id_type=MESH)
+    load.wait()
+    pl.semaphore_wait(barrier, len(order))
+
+    bag_copies = []
+    for mr in range(1, rows):
+        pr, _ = peer(mr, 0)
+        copy = pltpu.make_async_remote_copy(
+            src_ref=packed, dst_ref=gathered.at[r],
+            send_sem=bag_send.at[mr], recv_sem=bag_recv.at[mr],
+            device_id=(c, pr), device_id_type=MESH,
+        )
+        copy.start()
+        bag_copies.append(copy)
+
+    copies = []
+    for i, (mr, mc) in enumerate(order):
+        pr, pc = peer(mr, mc)
+        copy = pltpu.make_async_remote_copy(
+            src_ref=table_v.at[pl.ds((pc * rows + pr) * span, span), :],
+            dst_ref=out_ref.at[r, :, pl.ds(lane0, width)],
+            send_sem=send_sem.at[i], recv_sem=recv_sem.at[i],
+            device_id=(pc, pr), device_id_type=MESH,
+        )
+        copy.start()
+        copies.append((pr, pc, copy))
+
+    for copy in bag_copies:
+        copy.wait()
+
+    chunk = math.gcd(block_len, 16 * LANES)
+    lanes = lax.broadcasted_iota(jnp.int32, (tile_bags, chunk), 1)
+
+    def count(group, _):
+        shifted = gathered[group] - r * block_len
+        for q in range(per_vreg):
+            at = group * own_bags + q * tile_bags
+            for part in range(block_len // chunk):
+                here = shifted - part * chunk
+                total = jnp.zeros((tile_bags, chunk), jnp.float32)
+                for l in range(bag_len):
+                    lane = q * bag_len + l
+                    total += jnp.where(here[:, lane:lane + 1] == lanes, 1.0, 0.0)
+                counts[pl.ds(at, tile_bags), part * chunk:(part + 1) * chunk] = total
+        return 0
+
+    lax.fori_loop(0, rows, count, 0)
+
+    depth = math.gcd(block_len, 512)
+    partial[...] = jnp.zeros_like(partial)
+
+    def multiply(turn, _):
+        at = pl.multiple_of(turn * depth, depth)
+        block = table_v[pl.ds(at, depth), :]
+        times = counts[:, pl.ds(at, depth)].astype(jnp.bfloat16)
+        high = block.astype(jnp.bfloat16)
+        rest = block - high.astype(jnp.float32)
+        middle = rest.astype(jnp.bfloat16)
+        low = (rest - middle.astype(jnp.float32)).astype(jnp.bfloat16)
+        dot = functools.partial(jnp.dot, preferred_element_type=jnp.float32)
+        both = dot(times, jnp.concatenate([high, middle], axis=1))
+        step = (dot(times, low) + both[:, width:]) + both[:, :width]
+        partial[...] += step.reshape(partial.shape)
+        return 0
+
+    lax.fori_loop(0, block_len // depth, multiply, 0)
+
+    sum_copies = []
+    for mr in range(1, rows):
+        pr, _ = peer(mr, 0)
+        copy = pltpu.make_async_remote_copy(
+            src_ref=partial.at[pr], dst_ref=arrived.at[mr],
+            send_sem=sum_send.at[mr], recv_sem=sum_recv.at[mr],
+            device_id=(c, pr), device_id_type=MESH,
+        )
+        copy.start()
+        sum_copies.append(copy)
+
+    own.wait()
+    for copy in sum_copies:
+        copy.wait()
+    total = partial[r]
+    for mr in range(1, rows):
+        total += arrived[mr]
+    pooled_ref[...] = total
+    for pr, pc, copy in copies:
+        copy.wait()
+
+
+def ORDER(far, near):
+    return far + near
+
+
+def per_device(column_table, bag_rows):
+    rows, cols = lax.axis_size("row"), lax.axis_size("col")
+    block_len, width = column_table.shape
+    own_bags, bag_len = bag_rows.shape
+    span = block_len // (rows * cols)
+    fits = (
+        width % LANES == 0 and LANES % bag_len == 0 and own_bags * bag_len == SUBLANES * LANES
+        and span % SUBLANES == 0 and block_len % LANES == 0
+        and rows & (rows - 1) == 0 and cols & (cols - 1) == 0
+    )
+    if not fits:
+        return general(column_table, bag_rows)
+    bags = own_bags * rows
+    peers = rows * cols - 1
+    dma = pltpu.SemaphoreType.DMA
+    return pl.pallas_call(
+        functools.partial(kernel, rows, cols),
+        out_shape=(
+            jax.ShapeDtypeStruct((rows, span, width * cols), jnp.float32),
+            jax.ShapeDtypeStruct((own_bags, width), jnp.float32),
+        ),
+        in_specs=[pl.BlockSpec(memory_space=pltpu.HBM), pl.BlockSpec(memory_space=pltpu.VMEM)],
+        out_specs=(pl.BlockSpec(memory_space=pltpu.VMEM), pl.BlockSpec(memory_space=pltpu.VMEM)),
+        scratch_shapes=[
+            pltpu.VMEM((block_len, width), jnp.float32),
+            pltpu.VMEM((SUBLANES, LANES), jnp.int32),
+            pltpu.VMEM((rows, SUBLANES, LANES), jnp.int32),
+            pltpu.VMEM((bags, block_len), jnp.float32),
+            pltpu.VMEM((rows, own_bags, width), jnp.float32),
+            pltpu.VMEM((rows, own_bags, width), jnp.float32),
+            dma, dma, dma((peers,)), dma((peers,)),
+            dma((rows,)), dma((rows,)), dma((rows,)), dma((rows,)),
+        ],
+        compiler_params=pltpu.CompilerParams(
+            collective_id=0, has_side_effects=True, vmem_limit_bytes=32 * 1024 * 1024
+        ),
+    )(column_table, bag_rows)
+
+
 def solution(mesh):
     return jax.shard_map(
         per_device,

time: 162 us -> 67.1 us (0.41)
  waiting for transfers between devices: 63.8 us -> 0 us
  Pallas kernels: 0 us -> 62 us
  blocking collectives: 31.8 us -> 0 us
  other arithmetic: 22.3 us -> 0 us
  between operations: 14.1 us -> 0.65 us
  matrix products: 12.6 us -> 0 us
  starting transfers between devices: 9.69 us -> 0 us
  local copies, waits for them, and re-layouts: 6.71 us -> 4.23 us
    pallas_call x0 -> x1, Pallas kernels: none -> 62 us  [per_device(): pl.pallas_call(functools.partial(kernel, rows, cols), out_shape=(jax.Shap...]
    reduce_scatter x1 -> x0, waiting for transfers between devices: 56.6 us -> none  [per_device(): lax.psum_scatter(pooling(positions, column_table), 'row', scatter_dimensi...]
    all_gather x1 -> x0, blocking collectives: 31.8 us -> none  [per_device(): every_bag = lax.all_gather(bag_rows, 'row', axis=0, tiled=True)]
    reduce_sum x8 -> x0, other arithmetic: 22.2 us -> none  [advance(): counts = jnp.sum(matches.astype(jnp.float32), axis=1)]
    dot_general x8 -> x0, matrix products: 12.6 us -> none  [advance(): jnp.dot(counts, table_block, precision=lax.Precision.HIGHEST, preferred_e...]
    all_to_all x2 -> x0, starting transfers between devices: 9.66 us -> none  [the longest x1 5.38 us: per_device(): lax.all_to_all(lax.all_to_all(sectioned, 'col', split_axis=0, concat_axis...]
    all_to_all x2 -> x0, waiting for transfers between devices: 7.22 us -> none  [the longest x1 7.22 us: per_device(): lax.all_to_all(lax.all_to_all(sectioned, 'col', split_axis=0, concat_axis...]
    all_to_all x2 -> x0, local copies, waits for them, and re-layouts: 4.73 us -> none  [per_device(): lax.all_to_all(sectioned, 'col', split_axis=0, concat_axis=3, tiled=True)]
  transfers between devices with their start and end apart: 3 -> 0, of which waited for: 2 -> 0; matrix products, arithmetic and copies ran while one was open for 22% -> 0% of each run, Pallas kernels for 0% -> 0%
where the time goes in v1:
time: 67.1 us; the launch traced here: 66.9 us
  Pallas kernels  62 us (92%)
  local copies, waits for them, and re-layouts  4.23 us (6%)
    pallas_call x1, Pallas kernels, per_device(): pl.pallas_call(functools.partial(kernel, rows, cols), out_shape=(jax.Shap...  62 us
    unnamed x6, local copies, waits for them, and re-layouts  4.23 us

profile of v1, /device:TPU:0, one launch (start us, length us, event | category | flops | bytes accessed | tf_op | source)
XLA Modules:
  0.0 66.9 jit_solution(18182034204834298042)
XLA Ops:
  0.6 0.0 copy-start
  0.6 1.6 %copy-done = f32[4096,128]{1,0:T(8,128)S(1)} copy-done((f32[4096,128]{1,0:T(8,128)S(1)}, f32[4096,128]{1,0:T(8,128)}, u32[]{:S(2)}) %copy-start) | copy-done | bytes 2097176
  2.2 0.0 copy-start.1
  2.2 0.7 %copy-done.1 = s32[32,32]{1,0:T(8,128)S(1)} copy-done((s32[32,32]{1,0:T(8,128)S(1)}, s32[32,32]{1,0:T(8,128)}, u32[]{:S(2)}) %copy-start.1) | copy-done | bytes 4120
  2.9 62.0 %shard_map.41 = (f32[8,128,512]{2,1,0:T(8,128)S(1)}, f32[32,128]{1,0:T(8,128)S(1)}) custom-call(f32[4096,128]{1,0:T(8,128)S(1)} %copy-done, s32[32,32]{1,0:T(8,128)S(1)} %copy-done.1), custom_call_target="tpu_custom_call" | custom-call | tf_op jit(solution)/shard_map/pallas_call | solution.py:224
  65.0 1.3 %copy.6 = f32[8,128,512]{2,1,0:T(8,128)} copy(f32[8,128,512]{2,1,0:T(8,128)S(1)} %get-tuple-element.4) | data formatting | bytes 4194304
  66.3 0.6 copy.7
Async XLA Ops:
  0.6 1.6 %copy-start = (f32[4096,128]{1,0:T(8,128)S(1)}, f32[4096,128]{1,0:T(8,128)}, u32[]{:S(2)}) copy-start(f32[4096,128]{1,0:T(8,128)} %table_ref.1) | copy-start | bytes 6291460
  2.2 0.7 %copy-start.1 = (s32[32,32]{1,0:T(8,128)S(1)}, s32[32,32]{1,0:T(8,128)}, u32[]{:S(2)}) copy-start(s32[32,32]{1,0:T(8,128)} %bags_ref.1) | copy-start | bytes 12292

commit v2 on v1

--- a/solution.py
+++ b/solution.py
@@ -73,8 +73,8 @@
 def kernel(
     row_groups, col_groups,
     table_ref, bags_ref, out_ref, pooled_ref,
-    table_v, packed, gathered, counts, partial, arrived,
-    load_sem, own_sem, send_sem, recv_sem, bag_send, bag_recv, sum_send, sum_recv,
+    table_v, bags_v, packed, gathered, counts, partial, arrived, halves, crossed,
+    load_sem, bag_sem, own_sem, send_sem, recv_sem, bag_send, bag_recv, sum_send, sum_recv, cross_send, cross_recv,
 ):
     rows, cols = row_groups, col_groups
     r, c = lax.axis_index("row"), lax.axis_index("col")
@@ -84,6 +84,8 @@
     per_vreg = LANES // bag_len
     flat = c * rows + r
 
+    bag_load = pltpu.make_async_copy(bags_ref, bags_v, bag_sem)
+    bag_load.start()
     load = pltpu.make_async_copy(table_ref, table_v, load_sem)
     load.start()
     lane0 = pl.multiple_of(c * width, width)
@@ -94,18 +96,12 @@
     )
     own.start()
 
-    tile_bags = own_bags // per_vreg
-    packed[...] = jnp.concatenate(
-        [bags_ref[q * tile_bags:(q + 1) * tile_bags, :] for q in range(per_vreg)], axis=1
-    )
-    gathered[r] = packed[...]
-
     masks = [(mr, mc) for mr in range(rows) for mc in range(cols) if (mr, mc) != (0, 0)]
-    far = [m for m in masks if m[0] >= rows // 2]
-    near = [m for m in masks if m[0] < rows // 2]
-    far = sorted(far, key=lambda m: -m[0])
-    near = sorted(near, key=lambda m: -m[0])
-    order = ORDER(far, near)
+    half = rows // 2
+    far = [m for m in masks if m[0] >= half]
+    near = sorted((m for m in masks if m[0] < half), key=lambda m: -m[0])
+    order = [m for pair in zip(far, near + [None]) for m in pair if m]
+    cuts = [len(order) * n // 31 for n in CUTS]
 
     def peer(mr, mc):
         return flipped(r, mr, rows), flipped(c, mc, cols)
@@ -114,6 +110,12 @@
     for mr, mc in order:
         pr, pc = peer(mr, mc)
         pl.semaphore_signal(barrier, inc=1, device_id=(pc, pr), device_id_type=MESH)
+    bag_load.wait()
+    tile_bags = own_bags // per_vreg
+    packed[...] = jnp.concatenate(
+        [bags_v[q * tile_bags:(q + 1) * tile_bags, :] for q in range(per_vreg)], axis=1
+    )
+    gathered[r] = packed[...]
     load.wait()
     pl.semaphore_wait(barrier, len(order))
 
@@ -129,8 +131,14 @@
         bag_copies.append(copy)
 
     copies = []
-    for i, (mr, mc) in enumerate(order):
-        pr, pc = peer(mr, mc)
+
+    def send(first, last):
+        for i in range(first, last):
+            mr, mc = order[i]
+            pr, pc = peer(mr, mc)
+            send_one(i, pr, pc)
+
+    def send_one(i, pr, pc):
         copy = pltpu.make_async_remote_copy(
             src_ref=table_v.at[pl.ds((pc * rows + pr) * span, span), :],
             dst_ref=out_ref.at[r, :, pl.ds(lane0, width)],
@@ -138,7 +146,9 @@
             device_id=(pc, pr), device_id_type=MESH,
         )
         copy.start()
-        copies.append((pr, pc, copy))
+        copies.append(copy)
+
+    send(0, cuts[0])
 
     for copy in bag_copies:
         copy.wait()
@@ -160,6 +170,7 @@
         return 0
 
     lax.fori_loop(0, rows, count, 0)
+    send(cuts[0], cuts[1])
 
     depth = math.gcd(block_len, 512)
     partial[...] = jnp.zeros_like(partial)
@@ -180,30 +191,41 @@
 
     lax.fori_loop(0, block_len // depth, multiply, 0)
 
+    low, high = lax.rem(r, half), lax.div(r, half)
     sum_copies = []
-    for mr in range(1, rows):
+    for mr in range(1, half):
         pr, _ = peer(mr, 0)
         copy = pltpu.make_async_remote_copy(
-            src_ref=partial.at[pr], dst_ref=arrived.at[mr],
+            src_ref=partial.at[:, lax.rem(pr, half)], dst_ref=arrived.at[mr],
             send_sem=sum_send.at[mr], recv_sem=sum_recv.at[mr],
             device_id=(c, pr), device_id_type=MESH,
         )
         copy.start()
         sum_copies.append(copy)
-
-    own.wait()
+    send(cuts[1], cuts[2])
+
     for copy in sum_copies:
         copy.wait()
-    total = partial[r]
-    for mr in range(1, rows):
+    total = partial[:, low]
+    for mr in range(1, half):
         total += arrived[mr]
-    pooled_ref[...] = total
-    for pr, pc, copy in copies:
+    halves[...] = total
+    own.wait()
+    other, _ = peer(half, 0)
+    across = pltpu.make_async_remote_copy(
+        src_ref=halves.at[1 - high], dst_ref=crossed,
+        send_sem=cross_send, recv_sem=cross_recv,
+        device_id=(c, other), device_id_type=MESH,
+    )
+    across.start()
+    send(cuts[2], len(order))
+    across.wait()
+    pooled_ref[...] = halves[high] + crossed[...]
+    for copy in copies:
         copy.wait()
 
 
-def ORDER(far, near):
-    return far + near
+CUTS = (16, 21, 26)
 
 
 def per_device(column_table, bag_rows):
@@ -214,12 +236,13 @@
     fits = (
         width % LANES == 0 and LANES % bag_len == 0 and own_bags * bag_len == SUBLANES * LANES
         and span % SUBLANES == 0 and block_len % LANES == 0
-        and rows & (rows - 1) == 0 and cols & (cols - 1) == 0
+        and rows > 1 and rows & (rows - 1) == 0 and cols & (cols - 1) == 0
     )
     if not fits:
         return general(column_table, bag_rows)
     bags = own_bags * rows
     peers = rows * cols - 1
+    half = rows // 2
     dma = pltpu.SemaphoreType.DMA
     return pl.pallas_call(
         functools.partial(kernel, rows, cols),
@@ -227,22 +250,28 @@
             jax.ShapeDtypeStruct((rows, span, width * cols), jnp.float32),
             jax.ShapeDtypeStruct((own_bags, width), jnp.float32),
         ),
-        in_specs=[pl.BlockSpec(memory_space=pltpu.HBM), pl.BlockSpec(memory_space=pltpu.VMEM)],
+        in_specs=[pl.BlockSpec(memory_space=pltpu.HBM), pl.BlockSpec(memory_space=pltpu.HBM)],
         out_specs=(pl.BlockSpec(memory_space=pltpu.VMEM), pl.BlockSpec(memory_space=pltpu.VMEM)),
         scratch_shapes=[
             pltpu.VMEM((block_len, width), jnp.float32),
+            pltpu.VMEM((own_bags, bag_len), jnp.int32),
             pltpu.VMEM((SUBLANES, LANES), jnp.int32),
             pltpu.VMEM((rows, SUBLANES, LANES), jnp.int32),
             pltpu.VMEM((bags, block_len), jnp.float32),
-            pltpu.VMEM((rows, own_bags, width), jnp.float32),
-            pltpu.VMEM((rows, own_bags, width), jnp.float32),
-            dma, dma, dma((peers,)), dma((peers,)),
-            dma((rows,)), dma((rows,)), dma((rows,)), dma((rows,)),
+            pltpu.VMEM((2, half, own_bags, width), jnp.float32),
+            pltpu.VMEM((half, 2, own_bags, width), jnp.float32),
+            pltpu.VMEM((2, own_bags, width), jnp.float32),
+            pltpu.VMEM((own_bags, width), jnp.float32),
+            dma, dma, dma, dma((peers,)), dma((peers,)),
+            dma((rows,)), dma((rows,)), dma((half,)), dma((half,)), dma, dma,
         ],
         compiler_params=pltpu.CompilerParams(
             collective_id=0, has_side_effects=True, vmem_limit_bytes=32 * 1024 * 1024
         ),
-    )(column_table, bag_rows)
+    )(
+        pltpu.with_memory_space_constraint(column_table, pltpu.HBM),
+        pltpu.with_memory_space_constraint(bag_rows, pltpu.HBM),
+    )
 
 
 def solution(mesh):

time: 67.1 us -> 56.1 us (0.84)
  the two profiles are of different devices: /device:TPU:0 before, /device:TPU:9 now
where the time goes in v2:
time: 56.1 us; the launch traced here: 55.9 us
  Pallas kernels  53.3 us (95%)
  local copies, waits for them, and re-layouts  1.93 us (3%)
  between operations  0.64 us (1%)
    pallas_call x1, Pallas kernels, per_device(): pl.pallas_call(functools.partial(kernel, rows, cols), out_shape=(jax.Shap...  53.3 us
    unnamed x2, local copies, waits for them, and re-layouts  1.93 us

profile of v2, /device:TPU:9, one launch (start us, length us, event | category | flops | bytes accessed | tf_op | source)
XLA Modules:
  0.0 55.9 jit_solution(6653435564736024501)
XLA Ops:
  0.6 53.3 %shard_map.41 = (f32[8,128,512]{2,1,0:T(8,128)S(1)}, f32[32,128]{1,0:T(8,128)S(1)}) custom-call(f32[4096,128]{1,0:T(8,128)} %table_ref.1, s32[32,32]{1,0:T(8,128)} %bags_ref.1), custom_call_target="tpu_custom_call" | custom-call | tf_op jit(solution)/shard_map/pallas_call | solution.py:247
  53.9 1.3 %copy.6 = f32[8,128,512]{2,1,0:T(8,128)} copy(f32[8,128,512]{2,1,0:T(8,128)S(1)} %get-tuple-element.4) | data formatting | bytes 4194304
  55.2 0.6 %copy.7 = f32[32,128]{1,0:T(8,128)} copy(f32[32,128]{1,0:T(8,128)S(1)} %get-tuple-element.5) | data formatting | bytes 32768

commit v3 on v2

--- a/solution.py
+++ b/solution.py
@@ -88,10 +88,9 @@
     bag_load.start()
     load = pltpu.make_async_copy(table_ref, table_v, load_sem)
     load.start()
-    lane0 = pl.multiple_of(c * width, width)
     own = pltpu.make_async_copy(
         table_ref.at[pl.ds(flat * span, span), :],
-        out_ref.at[r, :, pl.ds(lane0, width)],
+        out_ref.at[r, c],
         own_sem,
     )
     own.start()
@@ -100,6 +99,7 @@
     half = rows // 2
     far = [m for m in masks if m[0] >= half]
     near = sorted((m for m in masks if m[0] < half), key=lambda m: -m[0])
+    far = sorted(far, key=lambda m: (m[0] >= half + half // 2, m[1], m[0]))
     order = [m for pair in zip(far, near + [None]) for m in pair if m]
     cuts = [len(order) * n // 31 for n in CUTS]
 
@@ -107,7 +107,7 @@
         return flipped(r, mr, rows), flipped(c, mc, cols)
 
     barrier = pltpu.get_barrier_semaphore()
-    for mr, mc in order:
+    for mr, mc in sorted(order, reverse=True):
         pr, pc = peer(mr, mc)
         pl.semaphore_signal(barrier, inc=1, device_id=(pc, pr), device_id_type=MESH)
     bag_load.wait()
@@ -141,7 +141,7 @@
     def send_one(i, pr, pc):
         copy = pltpu.make_async_remote_copy(
             src_ref=table_v.at[pl.ds((pc * rows + pr) * span, span), :],
-            dst_ref=out_ref.at[r, :, pl.ds(lane0, width)],
+            dst_ref=out_ref.at[r, c],
             send_sem=send_sem.at[i], recv_sem=recv_sem.at[i],
             device_id=(pc, pr), device_id_type=MESH,
         )
@@ -244,10 +244,10 @@
     peers = rows * cols - 1
     half = rows // 2
     dma = pltpu.SemaphoreType.DMA
-    return pl.pallas_call(
+    landed, sums = pl.pallas_call(
         functools.partial(kernel, rows, cols),
         out_shape=(
-            jax.ShapeDtypeStruct((rows, span, width * cols), jnp.float32),
+            jax.ShapeDtypeStruct((rows, cols, span, width), jnp.float32),
             jax.ShapeDtypeStruct((own_bags, width), jnp.float32),
         ),
         in_specs=[pl.BlockSpec(memory_space=pltpu.HBM), pl.BlockSpec(memory_space=pltpu.HBM)],
@@ -272,6 +272,30 @@
         pltpu.with_memory_space_constraint(column_table, pltpu.HBM),
         pltpu.with_memory_space_constraint(bag_rows, pltpu.HBM),
     )
+    return pl.pallas_call(
+        write_out,
+        out_shape=(
+            jax.ShapeDtypeStruct((rows, span, width * cols), jnp.float32),
+            jax.ShapeDtypeStruct((own_bags, width), jnp.float32),
+        ),
+        in_specs=[pl.BlockSpec(memory_space=pltpu.VMEM)] * 2,
+        out_specs=(pl.BlockSpec(memory_space=pltpu.HBM), pl.BlockSpec(memory_space=pltpu.HBM)),
+        scratch_shapes=[dma((cols,)), dma],
+        compiler_params=pltpu.CompilerParams(vmem_limit_bytes=8 * 1024 * 1024),
+    )(landed, sums)
+
+
+def write_out(landed_ref, sums_ref, out_ref, pooled_ref, sems, sum_sem):
+    rows, cols, _, width = landed_ref.shape
+    copies = [pltpu.make_async_copy(sums_ref, pooled_ref, sum_sem)]
+    for c in range(cols):
+        copies.append(pltpu.make_async_copy(
+            landed_ref.at[:, c], out_ref.at[:, :, c * width:(c + 1) * width], sems.at[c]
+        ))
+    for copy in copies:
+        copy.start()
+    for copy in copies:
+        copy.wait()
 
 
 def solution(mesh):

time: 56.1 us -> 55.8 us (level)
  local copies, waits for them, and re-layouts: 1.93 us -> 0 us
  Pallas kernels: 53.3 us -> 54.9 us
    unnamed x2 -> x0, local copies, waits for them, and re-layouts: 1.93 us -> none
    pallas_call x0 -> x1, Pallas kernels: none -> 1.36 us  [per_device(): pl.pallas_call(write_out, out_shape=(jax.ShapeDtypeStruct((rows, span, wi...]
where the time goes in v3:
time: 55.8 us; the launch traced here: 55.5 us
  Pallas kernels  54.9 us (98%)
  between operations  0.64 us (1%)
    pallas_call x1, Pallas kernels, per_device(): pl.pallas_call(functools.partial(kernel, rows, cols), out_shape=(jax.Shap...  53.5 us
    pallas_call x1, Pallas kernels, per_device(): pl.pallas_call(write_out, out_shape=(jax.ShapeDtypeStruct((rows, span, wi...  1.36 us

profile of v3, /device:TPU:9, one launch (start us, length us, event | category | flops | bytes accessed | tf_op | source)
XLA Modules:
  0.0 55.5 jit_solution(647431634948766555)
XLA Ops:
  0.6 53.5 %shard_map.41 = (f32[8,4,128,128]{3,2,1,0:T(8,128)S(1)}, f32[32,128]{1,0:T(8,128)S(1)}) custom-call(f32[4096,128]{1,0:T(8,128)} %table_ref.1, s32[32,32]{1,0:T(8,128)} %bags_ref.1), custom_call_target="tpu_custom_call" | custom-call | tf_op jit(solution)/shard_map/pallas_call | solution.py:247
  54.2 1.4 %shard_map.42 = (f32[8,128,512]{2,1,0:T(8,128)}, f32[32,128]{1,0:T(8,128)}) custom-call(f32[8,4,128,128]{3,2,1,0:T(8,128)S(1)} %get-tuple-element.4.landed_ref, f32[32,128]{1,0:T(8,128)S(1)} %get-tuple-element.5.sums_ref), custom_call_target="tpu_custom_call" | custom-call | tf_op jit(solution)/shard_map/pallas_call | solution.py:275
